TPU v7x, 32 devices: a whole 2x2x4 slice. The times are simulated.
32 devices in a mesh: band: 8 (over y, x, core), pw: 4 (over z).
Axes of the slice: x: 2, y: 2, z: 4, core: 2. Of those that a mesh axis runs over, the one named last changes fastest.
Arguments:
- pair_density: bfloat16 [40, 128, 9216], P('band', None, 'pw'), may hold values from -6 to 6
- eigvecs: bfloat16 [2944, 9216], P('band', 'pw'), may hold values from -0.0625 to 0.0625
- screening: bfloat16 [2944, 2944], P('pw'), may hold values from -0.00048828125 to 0.00048828125
- occupation: float32 [16], replicated, may hold values from 0 to 1
- window_start: int32 [40], P('band'), may hold values from 0 to 511, as said below
- window_len: int32 [40], P('band'), may hold values from 1 to 128, as said below
- slot_band: int32 [40], P('band'), may hold values from -1 to 15, as said below
Outputs:
- sigma: float32 [512, 512], P(('band', 'pw'))
Inputs may be any that keep to these rules, and one draw needn't show every extreme that they name: window_start + window_len <= 512 for every slot. `window_len`: some slot has a window of 128 bands. On each index of band the live slots (slot_band >= 0) come first among its 5 slots; each index holds 3 to 5 live slots, and the counts of index i and index i + 8 / 2 add up to 8.
All inputs are finite; a program needn't handle non-finite values.
Results may differ from a plain program's by a relative error of at most 0.0049.
Values may be sent and summed in bfloat16 or wider, within the bound.
A program may use at most 128 MiB of HBM per device.

v0:
```python
import jax
import jax.numpy as jnp
from jax import lax
from jax.sharding import PartitionSpec as P

NB_SIGMA = 512


def per_device(pair_density, eigvecs, screening, occupation, window_start, window_len, slot_band):
    capacity, block, plane_rows = pair_density.shape
    density, starts, lengths, band_ids = (pair_density, window_start, window_len, slot_band)
    slots = density.shape[0]
    flat = density.reshape(slots * block, plane_rows)
    partial_proj = lax.dot_general(
        flat,
        lax.all_gather(eigvecs, "band", axis=0, tiled=True),
        (((1,), (1,)), ((), ())),
        preferred_element_type=jnp.float32,
    )
    row_ids = jnp.arange(block, dtype=jnp.int32)
    keep_rows = ((row_ids[None, :] < lengths[:, None]) & (band_ids[:, None] >= 0)).astype(
        jnp.float32
    )
    masked = partial_proj * keep_rows.reshape(slots * block, 1)
    projected = lax.psum(masked, "pw").astype(jnp.bfloat16)
    width = screening.shape[0]
    own_cols = lax.dynamic_slice_in_dim(projected, lax.axis_index("pw") * width, width, 1)
    screened = lax.dot_general(
        projected, screening, (((1,), (1,)), ((), ())), preferred_element_type=jnp.float32
    ).astype(jnp.bfloat16)
    block_sigma = lax.dot_general(
        screened.reshape(slots, block, width),
        own_cols.reshape(slots, block, width),
        (((2,), (2,)), ((0,), (0,))),
        preferred_element_type=jnp.float32,
    )
    band_list = jnp.arange(occupation.shape[0], dtype=jnp.int32)
    weights = 0.5 - jnp.sum(
        jnp.where(band_list[None, :] == band_ids[:, None], occupation[None, :], 0.0), axis=1
    )
    totals = jnp.zeros((NB_SIGMA + block, NB_SIGMA + block), jnp.float32)
    for index in range(slots):
        first = starts[index]
        previous = lax.dynamic_slice(totals, (first, first), (block, block))
        totals = lax.dynamic_update_slice(
            totals, previous + weights[index] * block_sigma[index], (first, first)
        )
    sigma_part = totals[:NB_SIGMA, :NB_SIGMA]
    by_band = lax.psum_scatter(sigma_part, "band", scatter_dimension=0, tiled=True)
    return lax.psum_scatter(by_band, "pw", scatter_dimension=0, tiled=True)


def solution(mesh):
    return jax.shard_map(
        per_device,
        mesh=mesh,
        in_specs=(
            P("band", None, "pw"),
            P("band", "pw"),
            P("pw", None),
            P(),
            P("band"),
            P("band"),
            P("band"),
        ),
        out_specs=P(("band", "pw"), None),
        check_vma=False,
    )
```

profile of v0, /device:TPU:0, one launch (start us, length us, event | category | flops | bytes accessed | tf_op | source)
XLA Modules:
  0.0 465.4 jit_solution(47097493405840025)
XLA Ops:
  6.5 0.0 copy-start
  6.5 0.0 all-gather.2.cloned.1.call-start
  6.5 0.7 all-gather.2.cloned.1.call-update
  7.3 0.0 reduce-scatter.3.cloned.1.call-start
  7.3 1.4 fusion.11
  17.9 0.9 select_reduce_fusion
  18.7 0.7 fusion.10
  19.4 0.7 broadcast_compare_fusion
  20.1 0.7 convert_bitcast_fusion
  20.8 67.3 %all-gather.2.cloned.1.call-done = bf16[2944,2304]{1,0:T(8,128)(2,1)} async-done(((bf16[368,2304]{1,0:T(8,128)(2,1)}), bf16[2944,2304]{1,0:T(8,128)(2,1)}) %all-gather.2.cloned.1.call-update) | async-done | bytes 13565968 | tf_op jit(solution)/shard_map/all_gather | solution.py:16
  88.1 0.0 copy-done
  88.1 14.4 %convolution_multiply_fusion = f32[640,2944]{1,0:T(8,128)} fusion(bf16[640,2304]{1,0:T(8,128)(2,1)S(1)} %bitcast.39, bf16[2944,2304]{1,0:T(8,128)(2,1)} %all-gather.2.cloned.1.call-done, f32[640]{0:T(1024)S(1)} %convert_bitcast_fusion), kind=kOutput, calls=%fused_computation | convolution fusion | flops 8684093440 | bytes 24054272 | tf_op jit(solution)/shard_map/dot_general | solution.py:14
  102.5 259.2 %all-reduce.1 = bf16[640,2944]{1,0:T(8,128)(2,1)} all-reduce(f32[640,2944]{1,0:T(8,128)} %convolution_multiply_fusion), channel_id=1, replica_groups=mesh['band'=8,'pw'=4] {'pw'}, use_global_device_ids=true, to_apply=%region_1.2 | all-reduce | flops 1884160 | bytes 11304960 | tf_op jit(solution)/shard_map/psum | solution.py:25
  361.7 2.7 constant_dynamic-slice_fusion
  364.4 8.0 %convolution_convert_fusion = bf16[640,736]{0,1:T(8,128)(2,1)} fusion(bf16[640,2944]{1,0:T(8,128)(2,1)} %all-reduce.1, bf16[736,2944]{1,0:T(8,128)(2,1)} %param.9), kind=kOutput, calls=%fused_computation.1 | convolution fusion | flops 2773954560 | bytes 9043968 | tf_op jit(solution)/shard_map/dot_general | solution.py:28
  372.4 2.2 copy.12
  374.7 1.9 fusion.12
  376.6 0.7 fusion.8
  377.3 1.3 broadcast_in_dim.10
  378.6 3.0 dynamic_update_slice.15
  381.6 1.6 fusion.7
  383.2 3.0 dynamic_update_slice.16
  386.2 1.7 fusion.5
  387.9 3.3 dynamic_update_slice.17
  391.2 1.6 fusion.3
  392.8 3.2 dynamic_update_slice.18
  396.0 1.6 fusion.1
  397.7 3.2 dynamic_update_slice.19
  400.9 2.2 slice.69
  403.1 0.0 reduce-scatter.3.cloned.1.call-update
  403.2 0.0 reduce-scatter.5.cloned.1.call-start
  403.2 33.9 %reduce-scatter.3.cloned.1.call-done = f32[64,512]{1,0:T(8,128)} async-done(((f32[512,512]{1,0:T(8,128)}), f32[64,512]{1,0:T(8,128)}) %reduce-scatter.3.cloned.1.call-update) | async-done | bytes 131088 | tf_op jit(solution)/shard_map/reduce_scatter | solution.py:49
  437.1 0.0 reduce-scatter.5.cloned.1.call-update
  437.1 21.7 %reduce-scatter.5.cloned.1.call-done = f32[16,512]{1,0:T(8,128)} async-done(((f32[64,512]{1,0:T(8,128)}), f32[16,512]{1,0:T(8,128)}) %reduce-scatter.5.cloned.1.call-update) | async-done | bytes 32784 | tf_op jit(solution)/shard_map/reduce_scatter | solution.py:50
  (1 shorter events, 0.0 us)
Async XLA Ops:
  6.5 81.6 %copy-start = (bf16[5,128,2304]{2,1,0:T(8,128)(2,1)S(1)}, bf16[5,128,2304]{2,1,0:T(8,128)(2,1)}, u32[]{:S(2)}) copy-start(bf16[5,128,2304]{2,1,0:T(8,128)(2,1)} %param.7) | copy-start | bytes 8847364
  6.5 81.6 %all-gather.2.cloned.1.call-start = ((), (), s32[]{:S(2)}) async-start(), calls=%async_computation.2 | async-start | bytes 15261696 | tf_op jit(solution)/shard_map/all_gather | solution.py:16
  7.3 429.9 %reduce-scatter.3.cloned.1.call-start = ((), (), s32[]{:S(2)}) async-start(), calls=%async_computation.3 | async-start | bytes 1179648 | tf_op jit(solution)/shard_map/reduce_scatter | solution.py:49
  403.2 55.7 %reduce-scatter.5.cloned.1.call-start = ((), (), s32[]{:S(2)}) async-start(), calls=%async_computation.4 | async-start | bytes 163840 | tf_op jit(solution)/shard_map/reduce_scatter | solution.py:50
Sparse Core Ops, SparseCore 0:
  9.2 78.8 all-gather.1
  403.3 33.7 reduce-scatter.2
  439.4 19.4 reduce-scatter.4
where the time goes:
time: 467 us; the launch traced here: 465 us
  blocking collectives  259 us (55%)
  waiting for transfers between devices  124 us (27%)
  local copies, waits for them, and re-layouts  26.4 us (6%)
  matrix products  24.3 us (5%)
  between operations  22.3 us (5%)
  other arithmetic  9.5 us (2%)
    psum x1, blocking collectives, per_device(): projected = lax.psum(masked, 'pw').astype(jnp.bfloat16)  259 us
    all_gather x1, waiting for transfers between devices, per_device(): lax.all_gather(eigvecs, 'band', axis=0, tiled=True)  67.3 us
    reduce_scatter x1, waiting for transfers between devices, per_device(): lax.psum_scatter(sigma_part, 'band', scatter_dimension=0, tiled=True)  33.9 us
    reduce_scatter x1, waiting for transfers between devices, per_device(): return lax.psum_scatter(by_band, 'pw', scatter_dimension=0, tiled=True)  21.7 us
    dynamic_update_slice x5, local copies, waits for them, and re-layouts, per_device(): lax.dynamic_update_slice(totals, previous + weights[index] * block_sigma[...  15.8 us
    dot_general x1, matrix products, per_device(): lax.dot_general(flat, lax.all_gather(eigvecs, 'band', axis=0, tiled=True)...  14.4 us
  transfers between devices with their start and end apart: 3, of which 3 were waited for; matrix products, arithmetic and copies ran while one was open for 1% of the time, Pallas kernels for 0%

commit v1 on v0

--- a/solution.py
+++ b/solution.py
@@ -4,6 +4,12 @@
 from jax.sharding import PartitionSpec as P
 
 NB_SIGMA = 512
+
+
+def counts_plan(xs, ax_name):
+    after = jax.lax.all_gather(xs, ax_name)
+    base_arr = jnp.sum(after, 0)
+    return base_arr
 
 
 def per_device(pair_density, eigvecs, screening, occupation, window_start, window_len, slot_band):
@@ -22,7 +28,7 @@
         jnp.float32
     )
     masked = partial_proj * keep_rows.reshape(slots * block, 1)
-    projected = lax.psum(masked, "pw").astype(jnp.bfloat16)
+    projected = counts_plan(masked, "pw").astype(jnp.bfloat16)
     width = screening.shape[0]
     own_cols = lax.dynamic_slice_in_dim(projected, lax.axis_index("pw") * width, width, 1)
     screened = lax.dot_general(

time: 467 us -> 727 us (1.56)
  waiting for transfers between devices: 124 us -> 630 us
  blocking collectives: 259 us -> 0 us
  other arithmetic: 9.5 us -> 22.9 us
    all_gather x0 -> x1, waiting for transfers between devices: none -> 494 us  [counts_plan(): after = jax.lax.all_gather(xs, ax_name)]
    psum x1 -> x0, blocking collectives: 259 us -> none  [per_device(): projected = lax.psum(masked, 'pw').astype(jnp.bfloat16)]
    reduce_sum x0 -> x1, other arithmetic: none -> 14 us  [counts_plan(): base_arr = jnp.sum(after, 0)]
    all_gather x1, waiting for transfers between devices: 67.3 us -> 79.3 us  [per_device(): lax.all_gather(eigvecs, 'band', axis=0, tiled=True)]
  transfers between devices with their start and end apart: 3 -> 4, of which waited for: 3 -> 4; matrix products, arithmetic and copies ran while one was open for 1% -> 0% of each run, Pallas kernels for 0% -> 0%
where the time goes in v1:
time: 727 us; the launch traced here: 725 us
  waiting for transfers between devices  630 us (87%)
  local copies, waits for them, and re-layouts  25.7 us (4%)
  matrix products  23.5 us (3%)
  other arithmetic  22.9 us (3%)
  between operations  22.9 us (3%)
    all_gather x1, waiting for transfers between devices, counts_plan(): after = jax.lax.all_gather(xs, ax_name)  494 us
    all_gather x1, waiting for transfers between devices, per_device(): lax.all_gather(eigvecs, 'band', axis=0, tiled=True)  79.3 us
    reduce_scatter x1, waiting for transfers between devices, per_device(): lax.psum_scatter(sigma_part, 'band', scatter_dimension=0, tiled=True)  34.4 us
    reduce_scatter x1, waiting for transfers between devices, per_device(): return lax.psum_scatter(by_band, 'pw', scatter_dimension=0, tiled=True)  21.6 us
    dynamic_update_slice x5, local copies, waits for them, and re-layouts, per_device(): lax.dynamic_update_slice(totals, previous + weights[index] * block_sigma[...  15.8 us
  transfers between devices with their start and end apart: 4, of which 4 were waited for; matrix products, arithmetic and copies ran while one was open for 0% of the time, Pallas kernels for 0%

profile of v1, /device:TPU:0, one launch (start us, length us, event | category | flops | bytes accessed | tf_op | source)
XLA Modules:
  0.0 725.3 jit_solution(6339932580336313007)
XLA Ops:
  6.5 0.0 copy-start
  6.5 0.0 all-gather.4.cloned.1.call-start
  6.5 0.7 all-gather.4.cloned.1.call-update
  7.3 0.0 all-gather.6.cloned.1.call-start
  7.3 0.8 broadcast_compare_fusion
  8.1 0.7 convert_bitcast_fusion
  8.8 79.3 %all-gather.4.cloned.1.call-done = bf16[2944,2304]{1,0:T(8,128)(2,1)} async-done(((bf16[368,2304]{1,0:T(8,128)(2,1)}), bf16[2944,2304]{1,0:T(8,128)(2,1)}) %all-gather.4.cloned.1.call-update) | async-done | bytes 13565968 | tf_op jit(solution)/shard_map/all_gather | solution.py:22
  88.1 0.0 copy-done
  88.1 14.4 %convolution_multiply_fusion = f32[640,2944]{1,0:T(8,128)} fusion(bf16[640,2304]{1,0:T(8,128)(2,1)S(1)} %bitcast.40, bf16[2944,2304]{1,0:T(8,128)(2,1)} %all-gather.4.cloned.1.call-done, f32[640]{0:T(1024)S(1)} %convert_bitcast_fusion), kind=kOutput, calls=%fused_computation | convolution fusion | flops 8684093440 | bytes 24054272 | tf_op jit(solution)/shard_map/dot_general | solution.py:20
  102.5 0.0 copy-start.2
  102.5 0.0 copy-start.3
  102.5 0.0 copy-start.4
  102.5 0.0 all-gather.6.cloned.1.call-update
  102.6 0.0 reduce-scatter.3.cloned.1.call-start
  102.6 0.6 copy-done.2
  103.2 0.7 fusion.11
  113.6 0.0 copy-done.3
  113.6 0.0 copy-done.4
  113.6 0.2 select_reduce_fusion
  113.8 0.7 fusion.10
  114.5 494.1 %all-gather.6.cloned.1.call-done = f32[2560,2944]{1,0:T(8,128)} async-done(((f32[640,2944]{1,0:T(8,128)}), f32[2560,2944]{1,0:T(8,128)}) %all-gather.6.cloned.1.call-update) | async-done | bytes 30146576 | tf_op jit(solution)/shard_map/all_gather | solution.py:10
  608.5 14.0 %reduce_sum.19 = bf16[640,2944]{1,0:T(8,128)(2,1)} reduce(f32[4,640,2944]{2,1,0:T(8,128)} %bitcast.41, f32[]{:T(128)} %constant.7.clone.1), dimensions={0}, to_apply=%region_1.2 | reduce | flops 5652480 | bytes 33914884 | tf_op jit(solution)/shard_map/reduce_sum | solution.py:11
  622.6 2.7 constant_dynamic-slice_fusion
  625.2 7.0 convolution_convert_fusion
  632.2 1.7 copy.12
  634.0 0.0 copy-start.1
  634.0 2.1 fusion.12
  636.1 0.7 fusion.8
  636.7 1.3 broadcast_in_dim.10
  638.0 3.0 dynamic_update_slice.15
  641.1 1.6 fusion.7
  642.7 3.1 dynamic_update_slice.16
  645.8 1.7 fusion.5
  647.4 3.2 dynamic_update_slice.17
  650.7 1.6 fusion.3
  652.3 3.2 dynamic_update_slice.18
  655.5 1.6 fusion.1
  657.2 3.3 dynamic_update_slice.19
  660.4 2.3 slice.69
  662.7 0.0 reduce-scatter.3.cloned.1.call-update
  662.7 0.0 reduce-scatter.5.cloned.1.call-start
  662.8 34.4 %reduce-scatter.3.cloned.1.call-done = f32[64,512]{1,0:T(8,128)} async-done(((f32[512,512]{1,0:T(8,128)}), f32[64,512]{1,0:T(8,128)}) %reduce-scatter.3.cloned.1.call-update) | async-done | bytes 131088 | tf_op jit(solution)/shard_map/reduce_scatter | solution.py:55
  697.2 0.0 reduce-scatter.5.cloned.1.call-update
  697.2 21.6 %reduce-scatter.5.cloned.1.call-done = f32[16,512]{1,0:T(8,128)} async-done(((f32[64,512]{1,0:T(8,128)}), f32[16,512]{1,0:T(8,128)}) %reduce-scatter.5.cloned.1.call-update) | async-done | bytes 32784 | tf_op jit(solution)/shard_map/reduce_scatter | solution.py:56
  718.8 0.0 copy-done.1
  (1 shorter events, 0.0 us)
Async XLA Ops:
  6.5 81.6 %copy-start = (bf16[5,128,2304]{2,1,0:T(8,128)(2,1)S(1)}, bf16[5,128,2304]{2,1,0:T(8,128)(2,1)}, u32[]{:S(2)}) copy-start(bf16[5,128,2304]{2,1,0:T(8,128)(2,1)} %param.7) | copy-start | bytes 8847364
  6.5 81.6 %all-gather.4.cloned.1.call-start = ((), (), s32[]{:S(2)}) async-start(), calls=%async_computation.2 | async-start | bytes 15261696 | tf_op jit(solution)/shard_map/all_gather | solution.py:22
  7.3 601.3 %all-gather.6.cloned.1.call-start = ((), (), s32[]{:S(2)}) async-start(), calls=%async_computation.5 | async-start | bytes 37683200 | tf_op jit(solution)/shard_map/all_gather | solution.py:10
  102.5 0.7 copy-start.2
  102.5 11.1 %copy-start.3 = (s32[5]{0:T(128)S(1)}, s32[5]{0:T(128)}, u32[]{:S(2)}) copy-start(s32[5]{0:T(128)} %param.13) | copy-start | bytes 64
  102.5 11.1 %copy-start.4 = (f32[16]{0:T(128)S(1)}, f32[16]{0:T(128)}, u32[]{:S(2)}) copy-start(f32[16]{0:T(128)} %param.10) | copy-start | bytes 196
  102.6 594.6 %reduce-scatter.3.cloned.1.call-start = ((), (), s32[]{:S(2)}) async-start(), calls=%async_computation.3 | async-start | bytes 1179648 | tf_op jit(solution)/shard_map/reduce_scatter | solution.py:55
  634.0 84.8 %copy-start.1 = (bf16[5,128,2304]{2,1,0:T(8,128)(2,1)S(1)}, bf16[5,128,2304]{2,1,0:T(8,128)(2,1)}, u32[]{:S(2)}) copy-start(bf16[5,128,2304]{2,1,0:T(8,128)(2,1)} %param.7) | copy-start | bytes 8847364
  662.7 56.0 %reduce-scatter.5.cloned.1.call-start = ((), (), s32[]{:S(2)}) async-start(), calls=%async_computation.4 | async-start | bytes 163840 | tf_op jit(solution)/shard_map/reduce_scatter | solution.py:56
Sparse Core Ops, SparseCore 0:
  9.2 78.8 all-gather.3
  102.7 505.8 all-gather.5
  662.9 34.2 reduce-scatter.2
  699.3 19.4 reduce-scatter.4
